TPU v7x, 32 devices: a whole 2x2x4 slice. The times are simulated.
32 devices in a mesh: section: 2 (over core), dp: 8 (over z, x), mp: 2 (over y).
Axes of the slice: x: 2, y: 2, z: 4, core: 2. Of those that a mesh axis runs over, the one named last changes fastest.
Arguments:
- images: bfloat16 [2, 16, 197, 1024], P(None, 'dp'), may hold values from -6 to 6
- cotangent: bfloat16 [2, 16, 197, 1024], P(None, 'dp'), may hold values from -6 to 6
- live_count: int32 [2, 8], P(None, 'dp'), may hold values from 1 to 2, as said below
- ln1_gain: bfloat16 [2, 1024], P('section', 'dp'), may hold values from 0.099609375 to 1.8984375
- ln1_bias: bfloat16 [2, 1024], P('section', 'dp'), may hold values from -3 to 3
- qkv_weight: bfloat16 [2, 3, 1024, 1024], P('section', None, 'dp', 'mp'), may hold values from -0.1875 to 0.1875
- qv_bias: bfloat16 [2, 2, 16, 64], P('section', None, 'mp', 'dp'), may hold values from -3 to 3
- out_weight: bfloat16 [2, 1024, 1024], P('section', 'mp', 'dp'), may hold values from -1.5 to 1.5
- out_bias: bfloat16 [2, 1024], P('section', 'dp'), may hold values from -3 to 3
- ln2_gain: bfloat16 [2, 1024], P('section', 'dp'), may hold values from 0.099609375 to 1.8984375
- ln2_bias: bfloat16 [2, 1024], P('section', 'dp'), may hold values from -3 to 3
- up_weight: bfloat16 [2, 1024, 4096], P('section', 'dp', 'mp'), may hold values from -0.1875 to 0.1875
- up_bias: bfloat16 [2, 16, 256], P('section', 'mp', 'dp'), may hold values from -3 to 3
- down_weight: bfloat16 [2, 4096, 1024], P('section', 'mp', 'dp'), may hold values from -0.09375 to 0.09375
- down_bias: bfloat16 [2, 1024], P('section', 'dp'), may hold values from -3 to 3
Outputs:
- activations: bfloat16 [2, 2, 16, 197, 1024], P('section', None, 'dp')
- input_grads: bfloat16 [2, 2, 16, 197, 1024], P('section', None, 'dp')
- grad_ln1_gain: float32 [2, 1024], P('section', 'dp')
- grad_ln1_bias: float32 [2, 1024], P('section', 'dp')
- grad_qkv_weight: float32 [2, 3, 1024, 1024], P('section', None, 'dp', 'mp')
- grad_qv_bias: float32 [2, 2, 16, 64], P('section', None, 'mp', 'dp')
- grad_out_weight: float32 [2, 1024, 1024], P('section', 'mp', 'dp')
- grad_out_bias: float32 [2, 1024], P('section', 'dp')
- grad_ln2_gain: float32 [2, 1024], P('section', 'dp')
- grad_ln2_bias: float32 [2, 1024], P('section', 'dp')
- grad_up_weight: float32 [2, 1024, 4096], P('section', 'dp', 'mp')
- grad_up_bias: float32 [2, 16, 256], P('section', 'mp', 'dp')
- grad_down_weight: float32 [2, 4096, 1024], P('section', 'mp', 'dp')
- grad_down_bias: float32 [2, 1024], P('section', 'dp')
Inputs may be any that keep to these rules, and one draw needn't show every extreme that they name: Micro-batch m has live_count[m, d] images on data device d, in its first slots; its other slots hold values that no output reads.
All inputs are finite; a program needn't handle non-finite values.
Results may differ from a plain program's by a relative error of at most 0.015.
Values may be sent and summed in bfloat16 or wider, within the bound.
A program may use at most 256 MiB of HBM per device.

v0:
```python
import math
import jax
import jax.numpy as jnp
from jax import lax
from jax.sharding import PartitionSpec as P

HD = 64
epsilon = 1e-06


def gather_all(small, big):
    flat = jnp.concatenate([piece.reshape(-1) for piece in small])
    packed = lax.all_gather(flat, "dp", axis=0, tiled=False)
    count = packed.shape[0]
    whole, offset = ([], 0)
    for piece, axis in zip(small, (1, 1, 3, 1, 1, 1, 2, 1)):
        part = packed[:, offset : offset + piece.size].reshape((count,) + piece.shape)
        offset += piece.size
        part = jnp.moveaxis(part, 0, axis)
        shape = list(piece.shape)
        shape[axis] *= count
        whole.append(part.reshape(shape))
    qkv, out, up, down = (
        lax.all_gather(piece, "dp", axis=axis, tiled=True) for piece, axis in zip(big, (2, 2, 1, 2))
    )
    return (
        whole[0],
        whole[1],
        qkv,
        whole[2],
        out,
        whole[3],
        whole[4],
        whole[5],
        up,
        whole[6],
        down,
        whole[7],
    )


def scatter_all(totals, shards):
    small_at = (0, 1, 3, 5, 6, 7, 9, 11)
    count = lax.axis_size("dp")
    rows = []
    for index, axis in zip(small_at, (1, 1, 3, 1, 1, 1, 2, 1)):
        piece = totals[index]
        shape = list(piece.shape)
        shape[axis : axis + 1] = [count, shape[axis] // count]
        rows.append(jnp.moveaxis(piece.reshape(shape), axis, 0).reshape(count, -1))
    packed = lax.psum_scatter(jnp.concatenate(rows, axis=1), "dp", scatter_dimension=0, tiled=False)
    owned, offset = ([None] * 12, 0)
    for index in small_at:
        size = shards[index].size
        owned[index] = packed[offset : offset + size].reshape(shards[index].shape)
        offset += size
    for index, axis in zip((2, 4, 8, 10), (2, 2, 1, 2)):
        owned[index] = lax.psum_scatter(
            totals[index].astype(jnp.bfloat16), "dp", scatter_dimension=axis, tiled=True
        ).astype(jnp.float32)
    return owned


def both_halves(partial):
    return lax.psum(partial.astype(jnp.bfloat16), "mp").astype(jnp.float32)


def from_behind(x, axis, by):
    length = lax.axis_size(axis)
    pairs = [(i, i + by) for i in range(length) if 0 <= i + by < length]
    return lax.ppermute(x, axis, pairs)


def norm_parts(stream):
    centered = stream - jnp.mean(stream, axis=-1, keepdims=True)
    inverse = lax.rsqrt(jnp.mean(centered * centered, axis=-1, keepdims=True) + epsilon)
    return (centered * inverse, inverse)


def norm_back(grad_normed, normed, inverse):
    first_mean = jnp.mean(grad_normed, axis=-1, keepdims=True)
    second_mean = jnp.mean(grad_normed * normed, axis=-1, keepdims=True)
    return inverse * (grad_normed - first_mean - normed * second_mean)


def gelu_slope(preact):
    cumul = 0.5 * (1.0 + lax.erf(preact * 2.0 ** (-0.5)))
    density = jnp.exp(-0.5 * preact * preact) * (2.0 * math.pi) ** (-0.5)
    return cumul + preact * density


def unpack_weights(whole):
    return (
        whole[0][0].astype(jnp.float32),
        whole[1][0].astype(jnp.float32),
        whole[2][0],
        whole[3][0].reshape(2, -1).astype(jnp.float32),
        whole[4][0],
        whole[5][0].astype(jnp.float32),
        whole[6][0].astype(jnp.float32),
        whole[7][0].astype(jnp.float32),
        whole[8][0],
        whole[9][0].reshape(-1).astype(jnp.float32),
        whole[10][0],
        whole[11][0].astype(jnp.float32),
    )


def forward(stream, params, rows):
    (
        gain_one,
        shift_one,
        qkv_mat,
        qv_shift,
        out_mat,
        out_shift,
        gain_two,
        shift_two,
        up_mat,
        up_shift,
        down_mat,
        down_shift,
    ) = params
    batch_size, seq_len, model_width = stream.shape
    head_count = qkv_mat.shape[2] // HD
    scale = HD ** (-0.5)
    normed, inverse = norm_parts(stream)
    lowered = (normed * gain_one + shift_one).astype(jnp.bfloat16)
    projected = jnp.einsum("bld,cde->cble", lowered, qkv_mat, preferred_element_type=jnp.float32)
    split_shape = (batch_size, seq_len, head_count, HD)
    queries = (projected[0] + qv_shift[0]).astype(jnp.bfloat16).reshape(split_shape)
    keys_low = projected[1].astype(jnp.bfloat16).reshape(split_shape)
    values_low = (projected[2] + qv_shift[1]).astype(jnp.bfloat16).reshape(split_shape)
    scores = (
        jnp.einsum("blhe,bmhe->bhlm", queries, keys_low, preferred_element_type=jnp.float32) * scale
    )
    row_max = jnp.max(scores, axis=-1, keepdims=True)
    log_total = row_max + jnp.log(jnp.sum(jnp.exp(scores - row_max), axis=-1, keepdims=True))
    attn_probs = jnp.exp(scores - log_total)
    mixed = jnp.einsum(
        "bhlm,bmhe->blhe",
        attn_probs.astype(jnp.bfloat16),
        values_low,
        preferred_element_type=jnp.float32,
    )
    mixed = mixed.astype(jnp.bfloat16).reshape(batch_size, seq_len, -1)
    partial_attn = jnp.einsum("bld,de->ble", mixed, out_mat, preferred_element_type=jnp.float32)
    middle = stream + both_halves(partial_attn) + out_shift
    normed_two, inverse_two = norm_parts(middle)
    lowered_two = (normed_two * gain_two + shift_two).astype(jnp.bfloat16)
    preact = (
        jnp.einsum("bld,df->blf", lowered_two, up_mat, preferred_element_type=jnp.float32)
        + up_shift
    )
    gelu_out = jax.nn.gelu(preact, approximate=False).astype(jnp.bfloat16)
    partial_mlp = jnp.einsum("blf,fd->bld", gelu_out, down_mat, preferred_element_type=jnp.float32)
    result = (middle + both_halves(partial_mlp) + down_shift) * rows
    return (result, (stream, middle, queries, keys_low, values_low, log_total, mixed, preact))


def backward(seed, saved, params, shapes):
    (
        gain_one,
        shift_one,
        qkv_mat,
        qv_shift,
        out_mat,
        out_shift,
        gain_two,
        shift_two,
        up_mat,
        up_shift,
        down_mat,
        down_shift,
    ) = params
    stream, middle, queries, keys_low, values_low, log_total, mixed, preact = saved
    batch_size, seq_len, head_count, head_dim = queries.shape
    scale = HD ** (-0.5)
    normed, inverse = norm_parts(stream)
    lowered = (normed * gain_one + shift_one).astype(jnp.bfloat16)
    normed_two, inverse_two = norm_parts(middle)
    lowered_two = (normed_two * gain_two + shift_two).astype(jnp.bfloat16)
    gelu_out = jax.nn.gelu(preact, approximate=False).astype(jnp.bfloat16)
    grad_mlp = seed.astype(jnp.bfloat16)
    grad_down_shift = jnp.sum(grad_mlp.astype(jnp.float32), axis=(0, 1))
    grad_down_mat = jnp.einsum(
        "blf,bld->fd", gelu_out, grad_mlp, preferred_element_type=jnp.float32
    )
    grad_gelu = jnp.einsum("bld,fd->blf", grad_mlp, down_mat, preferred_element_type=jnp.float32)
    grad_pre = (grad_gelu * gelu_slope(preact)).astype(jnp.bfloat16)
    grad_up_shift = jnp.sum(grad_pre.astype(jnp.float32), axis=(0, 1))
    grad_up_mat = jnp.einsum(
        "bld,blf->df", lowered_two, grad_pre, preferred_element_type=jnp.float32
    )
    grad_low_two = both_halves(
        jnp.einsum("blf,df->bld", grad_pre, up_mat, preferred_element_type=jnp.float32)
    )
    grad_gain_two = jnp.sum(grad_low_two * normed_two, axis=(0, 1))
    grad_shift_two = jnp.sum(grad_low_two, axis=(0, 1))
    grad_middle = seed + norm_back(grad_low_two * gain_two, normed_two, inverse_two)
    grad_attn = grad_middle.astype(jnp.bfloat16)
    grad_out_shift = jnp.sum(grad_attn.astype(jnp.float32), axis=(0, 1))
    grad_out_mat = jnp.einsum("bld,ble->de", mixed, grad_attn, preferred_element_type=jnp.float32)
    grad_mixed = jnp.einsum("ble,de->bld", grad_attn, out_mat, preferred_element_type=jnp.float32)
    grad_mixed = grad_mixed.astype(jnp.bfloat16).reshape(batch_size, seq_len, head_count, head_dim)
    scores = (
        jnp.einsum("blhe,bmhe->bhlm", queries, keys_low, preferred_element_type=jnp.float32) * scale
    )
    attn_probs = jnp.exp(scores - log_total)
    grad_probs = jnp.einsum(
        "blhe,bmhe->bhlm", grad_mixed, values_low, preferred_element_type=jnp.float32
    )
    grad_values = jnp.einsum(
        "bhlm,blhe->bmhe",
        attn_probs.astype(jnp.bfloat16),
        grad_mixed,
        preferred_element_type=jnp.float32,
    ).astype(jnp.bfloat16)
    grad_scores = (
        attn_probs * (grad_probs - jnp.sum(attn_probs * grad_probs, axis=-1, keepdims=True))
    ).astype(jnp.bfloat16)
    grad_queries = (
        jnp.einsum("bhlm,bmhe->blhe", grad_scores, keys_low, preferred_element_type=jnp.float32)
        * scale
    ).astype(jnp.bfloat16)
    grad_keys = (
        jnp.einsum("bhlm,blhe->bmhe", grad_scores, queries, preferred_element_type=jnp.float32)
        * scale
    ).astype(jnp.bfloat16)
    grad_proj = jnp.stack([grad_queries, grad_keys, grad_values]).reshape(
        3, batch_size, seq_len, -1
    )
    grad_qv_shift = jnp.stack(
        [
            jnp.sum(grad_queries.astype(jnp.float32), axis=(0, 1)),
            jnp.sum(grad_values.astype(jnp.float32), axis=(0, 1)),
        ]
    )
    grad_qkv_mat = jnp.einsum(
        "bld,cble->cde", lowered, grad_proj, preferred_element_type=jnp.float32
    )
    grad_lowered = both_halves(
        jnp.einsum("cble,cde->bld", grad_proj, qkv_mat, preferred_element_type=jnp.float32)
    )
    grad_gain_one = jnp.sum(grad_lowered * normed, axis=(0, 1))
    grad_shift_one = jnp.sum(grad_lowered, axis=(0, 1))
    grad_stream = grad_middle + norm_back(grad_lowered * gain_one, normed, inverse)
    terms = [
        grad_gain_one,
        grad_shift_one,
        grad_qkv_mat,
        grad_qv_shift,
        grad_out_mat,
        grad_out_shift,
        grad_gain_two,
        grad_shift_two,
        grad_up_mat,
        grad_up_shift,
        grad_down_mat,
        grad_down_shift,
    ]
    return (grad_stream, [term.reshape(shape) for term, shape in zip(terms, shapes)])


def local(
    images,
    cotangent,
    live_count,
    ln1_gain,
    ln1_bias,
    qkv_weight,
    qv_bias,
    out_weight,
    out_bias,
    ln2_gain,
    ln2_bias,
    up_weight,
    up_bias,
    down_weight,
    down_bias,
):
    first_section = lax.axis_index("section") == 0
    micro_count = images.shape[0]
    slot_count = images.shape[1]
    slot_ids = jnp.arange(slot_count)
    small = (ln1_gain, ln1_bias, qv_bias, out_bias, ln2_gain, ln2_bias, up_bias, down_bias)
    gathered = gather_all(small, (qkv_weight, out_weight, up_weight, down_weight))
    params = unpack_weights(gathered)
    shapes = [piece.shape for piece in gathered]

    def row_mask(batch_index, valid):
        alive = jnp.logical_and(slot_ids < live_count[batch_index, 0], valid)
        return alive.astype(jnp.float32).reshape(slot_count, 1, 1)

    def choose(for_first, for_second):
        return jnp.where(first_section, for_first, for_second)

    incoming = jnp.zeros(images.shape[1:], jnp.bfloat16)
    outputs = []
    kept = []
    for moment in range(micro_count + 1):
        own = images[min(moment, micro_count - 1)]
        source = choose(own, incoming).astype(jnp.float32)
        rows = choose(
            row_mask(min(moment, micro_count - 1), moment < micro_count),
            row_mask(max(moment - 1, 0), moment >= 1),
        )
        result, saved = forward(source, params, rows)
        result = result.astype(jnp.bfloat16)
        outputs.append(result)
        kept.append(saved)
        if moment < micro_count:
            incoming = from_behind(result, "section", 1)
    activations = jnp.stack(
        [choose(outputs[index], outputs[index + 1]) for index in range(micro_count)]
    )
    totals = [jnp.zeros(shape, jnp.float32) for shape in shapes]
    incoming = jnp.zeros(images.shape[1:], jnp.bfloat16)
    returned = []
    for moment in range(micro_count + 1):
        later_index = min(moment, micro_count - 1)
        rows = choose(
            row_mask(max(moment - 1, 0), moment >= 1), row_mask(later_index, moment < micro_count)
        )
        seed = choose(incoming, cotangent[later_index]).astype(jnp.float32) * rows
        saved = jax.tree.map(choose, kept[max(moment - 1, 0)], kept[min(moment + 1, micro_count)])
        grad_stream, terms = backward(seed, saved, params, shapes)
        grad_low = grad_stream.astype(jnp.bfloat16)
        returned.append(grad_low)
        if moment < micro_count:
            incoming = from_behind(grad_low, "section", -1)
        totals = [first_part + second_part for first_part, second_part in zip(totals, terms)]
    shards = (
        ln1_gain,
        ln1_bias,
        qkv_weight,
        qv_bias,
        out_weight,
        out_bias,
        ln2_gain,
        ln2_bias,
        up_weight,
        up_bias,
        down_weight,
        down_bias,
    )
    owned = scatter_all(totals, shards)
    input_grads = jnp.stack(
        [choose(returned[index + 1], returned[index]) for index in range(micro_count)]
    )
    return (
        activations[None],
        input_grads[None],
        owned[0],
        owned[1],
        owned[2],
        owned[3],
        owned[4],
        owned[5],
        owned[6],
        owned[7],
        owned[8],
        owned[9],
        owned[10],
        owned[11],
    )


def solution(mesh):
    return jax.shard_map(
        local,
        mesh=mesh,
        in_specs=(
            P(None, "dp", None, None),
            P(None, "dp", None, None),
            P(None, "dp"),
            P("section", "dp"),
            P("section", "dp"),
            P("section", None, "dp", "mp"),
            P("section", None, "mp", "dp"),
            P("section", "mp", "dp"),
            P("section", "dp"),
            P("section", "dp"),
            P("section", "dp"),
            P("section", "dp", "mp"),
            P("section", "mp", "dp"),
            P("section", "mp", "dp"),
            P("section", "dp"),
        ),
        out_specs=(
            P("section", None, "dp", None, None),
            P("section", None, "dp", None, None),
            P("section", "dp"),
            P("section", "dp"),
            P("section", None, "dp", "mp"),
            P("section", None, "mp", "dp"),
            P("section", "mp", "dp"),
            P("section", "dp"),
            P("section", "dp"),
            P("section", "dp"),
            P("section", "dp", "mp"),
            P("section", "mp", "dp"),
            P("section", "mp", "dp"),
            P("section", "dp"),
        ),
        check_vma=False,
    )
```

profile of v0, /device:TPU:0, one launch (start us, length us, event | category | flops | bytes accessed | tf_op | source)
XLA Modules:
  0.0 1204.3 jit_solution(4596555902169269443)
XLA Ops:
  15.5 32.9 %all-gather.1 = bf16[8,1,1152]{2,1,0:T(2,128)(2,1)S(1)} all-gather(bf16[1,1,1152]{2,1,0:T(2,128)(2,1)S(1)} %reshape.803), channel_id=2, replica_groups=mesh['section'=2,'dp'=8,'mp'=2] {'dp'}, dimensions={0}, use_global_device_ids=true | all-gather | bytes 20736 | tf_op jit(solution)/shard_map/all_gather | solution.py:13
  52.2 20.9 %all-gather.7.cloned.1.call-done = bf16[1,3,1024,512]{3,2,1,0:T(8,128)(2,1)} async-done(((bf16[1,3,128,512]{3,2,1,0:T(8,128)(2,1)}), bf16[1,3,1024,512]{3,2,1,0:T(8,128)(2,1)}) %all-gather.7.cloned.1.call-update) | async-done | bytes 3145744 | tf_op jit(solution)/shard_map/all_gather | solution.py:24
  73.1 3.7 fusion.157
  87.2 26.0 %all-gather.9.cloned.1.call-done = bf16[1,512,1024]{2,1,0:T(8,128)(2,1)} async-done(((bf16[1,512,128]{2,1,0:T(8,128)(2,1)}), bf16[1,512,1024]{2,1,0:T(8,128)(2,1)}) %all-gather.9.cloned.1.call-update) | async-done | bytes 1048592 | tf_op jit(solution)/shard_map/all_gather | solution.py:24
  118.3 32.0 %all-reduce.14.cloned.1.call-done = bf16[2,197,1024]{2,1,0:T(8,128)(2,1)} async-done(((bf16[2,197,1024]{2,1,0:T(8,128)(2,1)}), bf16[2,197,1024]{2,1,0:T(8,128)(2,1)}) %all-reduce.14.cloned.1.call-update) | async-done | bytes 806928 | tf_op jit(solution)/shard_map/psum | solution.py:65
  153.7 71.4 %all-gather.11.cloned.1.call-done = bf16[1,1024,2048]{2,1,0:T(8,128)(2,1)} async-done(((bf16[1,128,2048]{2,1,0:T(8,128)(2,1)}), bf16[1,1024,2048]{2,1,0:T(8,128)(2,1)}) %all-gather.11.cloned.1.call-update) | async-done | bytes 4194320 | tf_op jit(solution)/shard_map/all_gather | solution.py:24
  225.1 7.2 fusion.571
  232.2 67.9 %all-gather.13.cloned.1.call-done = bf16[1,2048,1024]{2,1,0:T(8,128)(2,1)} async-done(((bf16[1,2048,128]{2,1,0:T(8,128)(2,1)}), bf16[1,2048,1024]{2,1,0:T(8,128)(2,1)}) %all-gather.13.cloned.1.call-update) | async-done | bytes 4194320 | tf_op jit(solution)/shard_map/all_gather | solution.py:24
  300.2 13.1 %fusion.460 = bf16[2,197,1024]{2,1,0:T(8,128)(2,1)} fusion(bf16[1,2048,1024]{2,1,0:T(8,128)(2,1)} %all-gather.13.cloned.1.call-done, f32[2,197,2048]{2,1,0:T(8,128)} %get-tuple-element.200, u8[197,2048]{1,0:T(8,128)(4,1)S(1)} %get-tuple-element.75, u8[197,2048]{1,0:T(8,128)(4,1)S(1)} %get-tuple-element.74), kind=kOutput, calls=%fused_computation.599 | convolution fusion | flops 1709443072 | bytes 9035776 | tf_op jit(solution)/shard_map/blf,fd->bld/dot_general | solution.py:156
  314.6 32.1 %all-reduce.16.cloned.1.call-done = bf16[2,197,1024]{2,1,0:T(8,128)(2,1)} async-done(((bf16[2,197,1024]{2,1,0:T(8,128)(2,1)}), bf16[2,197,1024]{2,1,0:T(8,128)(2,1)}) %all-reduce.16.cloned.1.call-update) | async-done | bytes 806928 | tf_op jit(solution)/shard_map/psum | solution.py:65
  372.0 32.1 %all-reduce.18.cloned.1.call-done = bf16[2,197,1024]{2,1,0:T(8,128)(2,1)} async-done(((bf16[2,197,1024]{2,1,0:T(8,128)(2,1)}), bf16[2,197,1024]{2,1,0:T(8,128)(2,1)}) %all-reduce.18.cloned.1.call-update) | async-done | bytes 806928 | tf_op jit(solution)/shard_map/psum | solution.py:65
  409.2 7.5 fusion.568
  416.7 4.5 convert_reduce_fusion.2
  424.0 11.5 fusion.465
  441.0 47.7 %all-reduce.30.cloned.1.call-done = (bf16[2,197,1024]{2,1,0:T(8,128)(2,1)}, bf16[2,197,1024]{2,1,0:T(8,128)(2,1)}) async-done(((bf16[2,197,1024]{2,1,0:T(8,128)(2,1)}, bf16[2,197,1024]{2,1,0:T(8,128)(2,1)}), (bf16[2,197,1024]{2,1,0:T(8,128)(2,1)}, bf16[2,197,1024]{2,1,0:T(8,128)(2,1)})) %all-reduce.30.cloned.1.call-update) | async-done | bytes 1613840 | tf_op jit(solution)/shard_map/psum | solution.py:65
  498.0 4.2 convert_reduce_fusion.22
  518.7 4.7 bitcast_convert_fusion.2
  543.1 3.6 fusion.611
  546.8 47.9 %all-reduce.28.cloned.1.call-done = (bf16[2,197,1024]{2,1,0:T(8,128)(2,1)}, bf16[2,197,1024]{2,1,0:T(8,128)(2,1)}) async-done(((bf16[2,197,1024]{2,1,0:T(8,128)(2,1)}, bf16[2,197,1024]{2,1,0:T(8,128)(2,1)}), (bf16[2,197,1024]{2,1,0:T(8,128)(2,1)}, bf16[2,197,1024]{2,1,0:T(8,128)(2,1)})) %all-reduce.28.cloned.1.call-update) | async-done | bytes 1613840 | tf_op jit(solution)/shard_map/psum | solution.py:65
  596.2 5.4 fusion.834
  605.4 10.2 fusion.569
  616.7 5.2 convert_reduce_fusion.1
  628.1 33.2 %all-reduce.20.cloned.1.call-done = bf16[2,197,1024]{2,1,0:T(8,128)(2,1)} async-done(((bf16[2,197,1024]{2,1,0:T(8,128)(2,1)}), bf16[2,197,1024]{2,1,0:T(8,128)(2,1)}) %all-reduce.20.cloned.1.call-update) | async-done | bytes 806928 | tf_op jit(solution)/shard_map/psum | solution.py:65
  671.9 4.4 convert_reduce_fusion.20
  688.8 4.6 bitcast_convert_fusion.1
  693.6 35.2 %all-reduce.22.cloned.1.call-done = bf16[2,197,1024]{2,1,0:T(8,128)(2,1)} async-done(((bf16[2,197,1024]{2,1,0:T(8,128)(2,1)}), bf16[2,197,1024]{2,1,0:T(8,128)(2,1)}) %all-reduce.22.cloned.1.call-update) | async-done | bytes 806928 | tf_op jit(solution)/shard_map/psum | solution.py:65
  749.7 13.1 %fusion.470 = bf16[2,197,1024]{2,1,0:T(8,128)(2,1)} fusion(bf16[1,2048,1024]{2,1,0:T(8,128)(2,1)} %all-gather.13.cloned.1.call-done, f32[2,197,2048]{2,1,0:T(8,128)} %get-tuple-element.208, u8[197,2048]{1,0:T(8,128)(4,1)} %get-tuple-element.150, u8[197,2048]{1,0:T(8,128)(4,1)} %get-tuple-element.151), kind=kOutput, calls=%fused_computation.601 | convolution fusion | flops 1709443072 | bytes 9035776 | tf_op jit(solution)/shard_map/blf,fd->bld/dot_general | solution.py:156
  763.2 22.6 %all-reduce.24.cloned.1.call-done = bf16[2,197,1024]{2,1,0:T(8,128)(2,1)} async-done(((bf16[2,197,1024]{2,1,0:T(8,128)(2,1)}), bf16[2,197,1024]{2,1,0:T(8,128)(2,1)}) %all-reduce.24.cloned.1.call-update) | async-done | bytes 806928 | tf_op jit(solution)/shard_map/psum | solution.py:65
  796.5 4.4 convert_reduce_fusion.18
  808.9 4.6 bitcast_convert_fusion
  815.1 3.6 fusion.604
  825.2 3.9 copy.285
  838.4 4.0 fusion.101
  842.4 7.8 copy.283
  850.2 5.0 copy.296
  855.4 11.3 fusion.169
  866.8 9.1 fusion.167
  875.9 10.6 fusion.100
  886.5 20.6 %copy.287 = bf16[1,2048,1024]{1,0,2:T(2,128)(2,1)} copy(bf16[1,2048,1024]{2,1,0:T(8,128)(2,1)} %fusion.100) | data formatting | bytes 8388608
  907.1 8.0 copy.409
  915.8 4.6 fusion.510
  920.4 5.9 fusion.511
  926.3 8.0 fusion.99
  939.2 3.7 fusion.515
  949.5 38.2 %all-reduce = f32[8,1152]{1,0:T(8,128)S(1)} all-reduce(f32[8,1152]{1,0:T(8,128)S(1)} %constant_dynamic-update-slice_fusion), channel_id=3, replica_groups=mesh['section'=2,'dp'=8,'mp'=2] {'dp'}, use_global_device_ids=true, to_apply=%region_84.85.clone | all-reduce | flops 9216 | bytes 73728
  993.0 19.8 %reduce-scatter.13.cloned.1.call-done = bf16[128,1536]{1,0:T(8,128)(2,1)} async-done(((bf16[1024,1536]{1,0:T(8,128)(2,1)}), bf16[128,1536]{1,0:T(8,128)(2,1)}) %reduce-scatter.13.cloned.1.call-update) | async-done | bytes 393232
  1015.9 87.8 %reduce-scatter.17.cloned.1.call-done = bf16[128,2048]{1,0:T(8,128)(2,1)} async-done(((bf16[1024,2048]{1,0:T(8,128)(2,1)}), bf16[128,2048]{1,0:T(8,128)(2,1)}) %reduce-scatter.17.cloned.1.call-update) | async-done | bytes 524304
  1107.3 87.8 %reduce-scatter.11.cloned.1.call-done = bf16[1,128,2048]{2,1,0:T(8,128)(2,1)} async-done(((bf16[1,1024,2048]{2,1,0:T(8,128)(2,1)}), bf16[1,128,2048]{2,1,0:T(8,128)(2,1)}) %reduce-scatter.11.cloned.1.call-update) | async-done | bytes 524304 | tf_op jit(solution)/shard_map/reduce_scatter | solution.py:58
  (644 shorter events, 234.1 us)
Async XLA Ops:
  7.2 65.9 %all-gather.7.cloned.1.call-start = ((), (), s32[]{:S(2)}) async-start(), calls=%async_computation.4 | async-start | bytes 3538944 | tf_op jit(solution)/shard_map/all_gather | solution.py:24
  7.9 105.3 %all-gather.9.cloned.1.call-start = ((), (), s32[]{:S(2)}) async-start(), calls=%async_computation.5 | async-start | bytes 1179648 | tf_op jit(solution)/shard_map/all_gather | solution.py:24
  8.7 141.6 %all-reduce.14.cloned.1.call-start = ((), (), s32[]{:S(2)}) async-start(), calls=%async_computation.6 | async-start | bytes 1638400 | tf_op jit(solution)/shard_map/psum | solution.py:65
  48.5 176.6 %copy-start.148 = (f32[1024]{0:T(1024)}, f32[1024]{0:T(1024)S(1)}, u32[]{:S(2)}) copy-start(f32[1024]{0:T(1024)S(1)} %get-tuple-element.190) | copy-start | bytes 12292
  48.5 298.2 %copy-start.112 = (f32[1024]{0:T(1024)}, f32[1024]{0:T(1024)S(1)}, u32[]{:S(2)}) copy-start(f32[1024]{0:T(1024)S(1)} %get-tuple-element.189) | copy-start | bytes 12292
  48.5 306.4 %copy-start.152 = (f32[1024]{0:T(1024)}, f32[1024]{0:T(1024)S(1)}, u32[]{:S(2)}) copy-start(f32[1024]{0:T(1024)S(1)} %get-tuple-element.194) | copy-start | bytes 12292
  48.5 556.9 %copy-start.103 = (f32[1024]{0:T(1024)}, f32[1024]{0:T(1024)S(1)}, u32[]{:S(2)}) copy-start(f32[1024]{0:T(1024)S(1)} %get-tuple-element.192) | copy-start | bytes 12292
  51.0 302.0 %copy-start.66 = (bf16[1,2,197,1024]{3,1,2,0:T(2,128)(2,1)}, bf16[1,2,197,1024]{3,1,2,0:T(2,128)(2,1)S(1)}, u32[]{:S(2)}) copy-start(bf16[1,2,197,1024]{3,1,2,0:T(2,128)(2,1)S(1)} %get-tuple-element.173) | copy-start | bytes 2420740
  52.1 306.7 %copy-start.110 = (f32[8,64]{1,0:T(8,128)}, f32[8,64]{1,0:T(8,128)S(1)}, u32[]{:S(2)}) copy-start(f32[8,64]{1,0:T(8,128)S(1)} %add.600) | copy-start | bytes 6148
  52.2 309.4 %copy-start.108 = (f32[8,64]{1,0:T(8,128)}, f32[8,64]{1,0:T(8,128)S(1)}, u32[]{:S(2)}) copy-start(f32[8,64]{1,0:T(8,128)S(1)} %add.603) | copy-start | bytes 6148
  86.4 29.5 %copy-start.51 = (bf16[2,197,8,64]{1,3,2,0:T(8,128)(2,1)}, bf16[2,197,8,64]{1,3,2,0:T(8,128)(2,1)S(1)}, u32[]{:S(2)}) copy-start(bf16[2,197,8,64]{1,3,2,0:T(8,128)(2,1)S(1)} %add_convert_fusion.14) | copy-start | bytes 1210372
  87.2 66.5 %copy-start.79 = (bf16[2,8,64,197]{3,2,1,0:T(8,128)(2,1)}, bf16[2,8,64,197]{3,2,1,0:T(8,128)(2,1)S(1)}, u32[]{:S(2)}) copy-start(bf16[2,8,64,197]{3,2,1,0:T(8,128)(2,1)S(1)} %fusion.484) | copy-start | bytes 1210372
  116.0 109.1 %all-gather.11.cloned.1.call-start = ((), (), s32[]{:S(2)}) async-start(), calls=%async_computation.7 | async-start | bytes 4718592 | tf_op jit(solution)/shard_map/all_gather | solution.py:24
  116.6 183.6 %all-gather.13.cloned.1.call-start = ((), (), s32[]{:S(2)}) async-start(), calls=%async_computation.8 | async-start | bytes 4718592 | tf_op jit(solution)/shard_map/all_gather | solution.py:24
  117.2 229.5 %all-reduce.16.cloned.1.call-start = ((), (), s32[]{:S(2)}) async-start(), calls=%async_computation.9 | async-start | bytes 1638400 | tf_op jit(solution)/shard_map/psum | solution.py:65
  118.3 114.0 %copy-start.160 = (f32[2048]{0:T(1024)}, f32[2048]{0:T(1024)S(1)}, u32[]{:S(2)}) copy-start(f32[2048]{0:T(1024)S(1)} %reshape.797) | copy-start | bytes 24580
  150.3 74.8 %copy-start.15 = (bf16[2,197,1024]{2,1,0:T(8,128)(2,1)S(1)}, bf16[2,197,1024]{2,1,0:T(8,128)(2,1)}, u32[]{:S(2)}) copy-start(bf16[2,197,1024]{2,1,0:T(8,128)(2,1)} %all-reduce.14.cloned.1.call-done) | copy-start | bytes 2420740
  300.2 13.2 %copy-start.166 = (s32[2,1]{0,1:T(1,128)S(1)}, s32[2,1]{0,1:T(1,128)}, u32[]{:S(2)}) copy-start(s32[2,1]{0,1:T(1,128)} %param.17) | copy-start | bytes 28
  313.3 90.8 %all-reduce.18.cloned.1.call-start = ((), (), s32[]{:S(2)}) async-start(), calls=%async_computation.10 | async-start | bytes 1638400 | tf_op jit(solution)/shard_map/psum | solution.py:65
  349.3 3.6 collective-permute-start
  368.8 119.8 %all-reduce.30.cloned.1.call-start = ((), (), s32[]{:S(2)}) async-start(), calls=%async_computation.20 | async-start | bytes 3276800 | tf_op jit(solution)/shard_map/psum | solution.py:65
  369.7 121.6 %copy-start.167 = (f32[2]{0:T(128)}, f32[2]{0:T(128)S(1)}, u32[]{:S(2)}) copy-start(f32[2]{0:T(128)S(1)} %broadcast_select_fusion.29) | copy-start | bytes 28
  372.0 37.1 %copy-start.119 = (f32[2,197]{1,0:T(2,128)}, f32[2,197]{1,0:T(2,128)S(1)}, u32[]{:S(2)}) copy-start(f32[2,197]{1,0:T(2,128)S(1)} %broadcast_multiply_fusion.14) | copy-start | bytes 4732
  372.0 37.1 %copy-start.149 = (f32[1024]{0:T(1024)S(1)}, f32[1024]{0:T(1024)}, u32[]{:S(2)}) copy-start(f32[1024]{0:T(1024)} %copy-done.148) | copy-start | bytes 12292
  372.0 37.1 %copy-start.161 = (f32[2048]{0:T(1024)S(1)}, f32[2048]{0:T(1024)}, u32[]{:S(2)}) copy-start(f32[2048]{0:T(1024)} %copy-done.160) | copy-start | bytes 24580
  409.1 82.2 %copy-start.6 = (f32[2,197,1024]{2,1,0:T(8,128)}, f32[2,197,1024]{2,1,0:T(8,128)S(1)}, u32[]{:S(2)}) copy-start(f32[2,197,1024]{2,1,0:T(8,128)S(1)} %get-tuple-element.145) | copy-start | bytes 4841476
  435.5 159.2 %all-reduce.28.cloned.1.call-start = ((), (), s32[]{:S(2)}) async-start(), calls=%async_computation.19 | async-start | bytes 3276800 | tf_op jit(solution)/shard_map/psum | solution.py:65
  440.6 53.5 %copy-start.115 = (f32[2,197]{1,0:T(2,128)}, f32[2,197]{1,0:T(2,128)S(1)}, u32[]{:S(2)}) copy-start(f32[2,197]{1,0:T(2,128)S(1)} %broadcast_multiply_fusion.17) | copy-start | bytes 4732
  441.0 53.2 %copy-start.121 = (f32[2,197]{1,0:T(2,128)}, f32[2,197]{1,0:T(2,128)S(1)}, u32[]{:S(2)}) copy-start(f32[2,197]{1,0:T(2,128)S(1)} %add_rsqrt_fusion.5) | copy-start | bytes 4732
  507.3 16.0 %collective-permute-start.1 = (bf16[2,197,1024]{2,0,1:T(2,128)(2,1)}, bf16[2,197,1024]{2,0,1:T(2,128)(2,1)}, u32[]{:S(2)}, u32[]{:S(2)}) collective-permute-start(bf16[2,197,1024]{2,0,1:T(2,128)(2,1)} %copy.214), channel_id=1, source_target_pairs={{0,16},{1,17},{2,18},{3,19},{4,20},{5,21},{6,22},{7,23},{8,24},{9,... | collective-permute-start | bytes 2420744 | tf_op jit(solution)/shard_map/ppermute | solution.py:71
  541.5 119.7 %all-reduce.20.cloned.1.call-start = ((), (), s32[]{:S(2)}) async-start(), calls=%async_computation.11 | async-start | bytes 1638400 | tf_op jit(solution)/shard_map/psum | solution.py:65
  543.1 58.5 %copy-start.127 = (f32[2,197]{1,0:T(2,128)}, f32[2,197]{1,0:T(2,128)S(1)}, u32[]{:S(2)}) copy-start(f32[2,197]{1,0:T(2,128)S(1)} %add_rsqrt_fusion.4) | copy-start | bytes 4732
  543.1 53.1 %copy-start.16 = (bf16[2,197,1024]{2,1,0:T(8,128)(2,1)S(1)}, bf16[2,197,1024]{2,1,0:T(8,128)(2,1)}, u32[]{:S(2)}) copy-start(bf16[2,197,1024]{2,1,0:T(8,128)(2,1)} %all-reduce.14.cloned.1.call-done) | copy-start | bytes 2420740
  543.1 53.1 %copy-start.120 = (f32[2,197]{1,0:T(2,128)S(1)}, f32[2,197]{1,0:T(2,128)}, u32[]{:S(2)}) copy-start(f32[2,197]{1,0:T(2,128)} %copy-done.119) | copy-start | bytes 4732
  603.8 12.9 %copy-start.170 = (bf16[1,2048,1024]{2,1,0:T(8,128)(2,1)S(1)}, bf16[1,2048,1024]{2,1,0:T(8,128)(2,1)}, u32[]{:S(2)}) copy-start(bf16[1,2048,1024]{2,1,0:T(8,128)(2,1)} %all-gather.13.cloned.1.call-done) | copy-start | bytes 12582916
  603.8 11.8 collective-permute-start.2
  626.0 102.7 %all-reduce.22.cloned.1.call-start = ((), (), s32[]{:S(2)}) async-start(), calls=%async_computation.12 | async-start | bytes 1638400 | tf_op jit(solution)/shard_map/psum | solution.py:65
  626.3 41.1 %copy-start.117 = (f32[2,197]{1,0:T(2,128)}, f32[2,197]{1,0:T(2,128)S(1)}, u32[]{:S(2)}) copy-start(f32[2,197]{1,0:T(2,128)S(1)} %broadcast_multiply_fusion.11) | copy-start | bytes 4732
  628.0 39.3 %copy-start.123 = (f32[2,197]{1,0:T(2,128)}, f32[2,197]{1,0:T(2,128)S(1)}, u32[]{:S(2)}) copy-start(f32[2,197]{1,0:T(2,128)S(1)} %add_rsqrt_fusion.3) | copy-start | bytes 4732
  693.5 92.3 %all-reduce.24.cloned.1.call-start = ((), (), s32[]{:S(2)}) async-start(), calls=%async_computation.13 | async-start | bytes 1638400 | tf_op jit(solution)/shard_map/psum | solution.py:65
  693.6 40.6 %copy-start.125 = (f32[2,197]{1,0:T(2,128)}, f32[2,197]{1,0:T(2,128)S(1)}, u32[]{:S(2)}) copy-start(f32[2,197]{1,0:T(2,128)S(1)} %add_rsqrt_fusion.2) | copy-start | bytes 4732
  735.0 4.8 collective-permute-start.3
  749.7 187.3 %all-reduce.26.cloned.1.call-start = ((), (), s32[]{:S(2)}) async-start(), calls=%async_computation.18 | async-start | bytes 3276800 | tf_op jit(solution)/shard_map/psum | solution.py:65
  749.7 13.1 %copy-start.3 = (f32[2,197,1024]{2,1,0:T(8,128)S(1)}, f32[2,197,1024]{2,1,0:T(8,128)}, u32[]{:S(2)}) copy-start(f32[2,197,1024]{2,1,0:T(8,128)} %get-tuple-element.137) | copy-start | bytes 4841476
  813.5 177.6 %reduce-scatter.15.cloned.1.call-start = ((), (), s32[]{:S(2)}) async-start(), calls=%async_computation.16 | async-start | bytes 1179648
  832.1 180.8 %reduce-scatter.13.cloned.1.call-start = ((), (), s32[]{:S(2)}) async-start(), calls=%async_computation.15 | async-start | bytes 3538944
  855.3 248.5 %reduce-scatter.17.cloned.1.call-start = ((), (), s32[]{:S(2)}) async-start(), calls=%async_computation.17 | async-start | bytes 4718592
  915.1 280.0 %reduce-scatter.11.cloned.1.call-start = ((), (), s32[]{:S(2)}) async-start(), calls=%async_computation.14 | async-start | bytes 4718592 | tf_op jit(solution)/shard_map/reduce_scatter | solution.py:58
  (163 other events, 647.9 us)
Sparse Core Ops, SparseCore 0:
  10.2 62.8 all-gather.6
  75.1 38.0 all-gather.8
  116.1 34.0 all-reduce.13
  152.2 72.7 all-gather.10
  227.0 73.1 all-gather.12
  313.4 33.2 all-reduce.15
  369.0 35.1 all-reduce.17
  435.6 52.9 all-reduce.29
  541.7 52.9 all-reduce.27
  626.1 35.0 all-reduce.19
  693.6 35.0 all-reduce.21
  749.8 35.9 all-reduce.23
  813.7 52.9 all-reduce.25
  870.5 64.1 reduce-scatter.14
  938.2 74.6 reduce-scatter.12
  1016.3 87.3 reduce-scatter.16
  1107.2 87.9 reduce-scatter.10
where the time goes:
time: 1210 us; the launch traced here: 1200 us
  waiting for transfers between devices  669 us (55%)
  matrix products  222 us (18%)
  local copies, waits for them, and re-layouts  137 us (11%)
  other arithmetic  78.5 us (6%)
  blocking collectives  71.1 us (6%)
  between operations  16.9 us (1%)
    psum x9, waiting for transfers between devices, both_halves(): return lax.psum(partial.astype(jnp.bfloat16), 'mp').astype(jnp.float32)  283 us
    all_gather x4, waiting for transfers between devices, gather_all(): lax.all_gather(piece, 'dp', axis=axis, tiled=True)  186 us
    unnamed x20, waiting for transfers between devices  110 us
    reduce_scatter x1, waiting for transfers between devices, scatter_all(): lax.psum_scatter(totals[index].astype(jnp.bfloat16), 'dp', scatter_dimens...  87.8 us
    unnamed x407, local copies, waits for them, and re-layouts  79.7 us
    unnamed x1, blocking collectives  38.2 us
    dot_general x3, matrix products, forward(): jnp.einsum('blf,fd->bld', gelu_out, down_mat, preferred_element_type=jnp....  37.7 us
    all_gather x1, blocking collectives, gather_all(): packed = lax.all_gather(flat, 'dp', axis=0, tiled=False)  32.9 us
  transfers between devices with their start and end apart: 21, of which 16 were waited for; matrix products, arithmetic and copies ran while one was open for 20% of the time, Pallas kernels for 0%

commit v1 on v0

--- a/solution.py
+++ b/solution.py
@@ -62,7 +62,7 @@
 
 
 def both_halves(partial):
-    return lax.psum(partial.astype(jnp.bfloat16), "mp").astype(jnp.float32)
+    return jnp.sum(lax.all_gather(partial.astype(jnp.bfloat16), "mp"), axis=0).astype(jnp.float32)
 
 
 def from_behind(x, axis, by):

time: 1210 us -> 1140 us (0.942)
  waiting for transfers between devices: 669 us -> 540 us
  other arithmetic: 78.5 us -> 115 us
  matrix products: 222 us -> 236 us
    psum x9 -> x0, waiting for transfers between devices: 283 us -> none  [both_halves(): return lax.psum(partial.astype(jnp.bfloat16), 'mp').astype(jnp.float32)]
    all_gather x0 -> x12, waiting for transfers between devices: none -> 187 us  [both_halves(): lax.all_gather(partial.astype(jnp.bfloat16), 'mp')]
    reduce_sum x0 -> x12, other arithmetic: none -> 33.5 us  [both_halves(): jnp.sum(lax.all_gather(partial.astype(jnp.bfloat16), 'mp'), axis=0)]
    unnamed x20 -> x23, waiting for transfers between devices: 110 us -> 77.9 us
    unnamed x407 -> x361, local copies, waits for them, and re-layouts: 79.7 us -> 80.3 us
  transfers between devices with their start and end apart: 21 -> 24, of which waited for: 16 -> 18; matrix products, arithmetic and copies ran while one was open for 20% -> 30% of each run, Pallas kernels for 0% -> 0%
where the time goes in v1:
time: 1140 us; the launch traced here: 1130 us
  waiting for transfers between devices  540 us (47%)
  matrix products  236 us (21%)
  local copies, waits for them, and re-layouts  145 us (13%)
  other arithmetic  115 us (10%)
  blocking collectives  71.1 us (6%)
  between operations  16.6 us (1%)
    all_gather x12, waiting for transfers between devices, both_halves(): lax.all_gather(partial.astype(jnp.bfloat16), 'mp')  187 us
    all_gather x4, waiting for transfers between devices, gather_all(): lax.all_gather(piece, 'dp', axis=axis, tiled=True)  185 us
    reduce_scatter x1, waiting for transfers between devices, scatter_all(): lax.psum_scatter(totals[index].astype(jnp.bfloat16), 'dp', scatter_dimens...  87.9 us
    unnamed x361, local copies, waits for them, and re-layouts  80.3 us
    unnamed x23, waiting for transfers between devices  77.9 us
    dot_general x3, matrix products, forward(): jnp.einsum('blf,fd->bld', gelu_out, down_mat, preferred_element_type=jnp....  38.8 us
    unnamed x1, blocking collectives  38.2 us
    reduce_sum x12, other arithmetic, both_halves(): jnp.sum(lax.all_gather(partial.astype(jnp.bfloat16), 'mp'), axis=0)  33.5 us
  transfers between devices with their start and end apart: 24, of which 18 were waited for; matrix products, arithmetic and copies ran while one was open for 30% of the time, Pallas kernels for 0%

profile of v1, /device:TPU:0, one launch (start us, length us, event | category | flops | bytes accessed | tf_op | source)
XLA Modules:
  0.0 1133.7 jit_solution(5799825334629804833)
XLA Ops:
  15.5 32.9 %all-gather.13 = bf16[8,1,1152]{2,1,0:T(2,128)(2,1)S(1)} all-gather(bf16[1,1,1152]{2,1,0:T(2,128)(2,1)S(1)} %reshape.826), channel_id=2, replica_groups=mesh['section'=2,'dp'=8,'mp'=2] {'dp'}, dimensions={0}, use_global_device_ids=true | all-gather | bytes 20736 | tf_op jit(solution)/shard_map/all_gather | solution.py:13
  53.3 19.8 %all-gather.31.cloned.1.call-done = bf16[1,3,1024,512]{3,2,1,0:T(8,128)(2,1)} async-done(((bf16[1,3,128,512]{3,2,1,0:T(8,128)(2,1)}), bf16[1,3,1024,512]{3,2,1,0:T(8,128)(2,1)}) %all-gather.31.cloned.1.call-update) | async-done | bytes 3145744 | tf_op jit(solution)/shard_map/all_gather | solution.py:24
  87.2 26.0 %all-gather.33.cloned.1.call-done = bf16[1,512,1024]{2,1,0:T(8,128)(2,1)} async-done(((bf16[1,512,128]{2,1,0:T(8,128)(2,1)}), bf16[1,512,1024]{2,1,0:T(8,128)(2,1)}) %all-gather.33.cloned.1.call-update) | async-done | bytes 1048592 | tf_op jit(solution)/shard_map/all_gather | solution.py:24
  117.6 25.5 %all-gather.39.cloned.1.call-done = bf16[4,197,1024]{2,1,0:T(8,128)(2,1)} async-done(((bf16[2,197,1024]{2,1,0:T(8,128)(2,1)}), bf16[4,197,1024]{2,1,0:T(8,128)(2,1)}) %all-gather.39.cloned.1.call-update) | async-done | bytes 1613840 | tf_op jit(solution)/shard_map/all_gather | solution.py:65
  146.3 71.7 %all-gather.35.cloned.1.call-done = bf16[1,1024,2048]{2,1,0:T(8,128)(2,1)} async-done(((bf16[1,128,2048]{2,1,0:T(8,128)(2,1)}), bf16[1,1024,2048]{2,1,0:T(8,128)(2,1)}) %all-gather.35.cloned.1.call-update) | async-done | bytes 4194320 | tf_op jit(solution)/shard_map/all_gather | solution.py:24
  217.9 7.2 fusion.583
  225.1 67.9 %all-gather.37.cloned.1.call-done = bf16[1,2048,1024]{2,1,0:T(8,128)(2,1)} async-done(((bf16[1,2048,128]{2,1,0:T(8,128)(2,1)}), bf16[1,2048,1024]{2,1,0:T(8,128)(2,1)}) %all-gather.37.cloned.1.call-update) | async-done | bytes 4194320 | tf_op jit(solution)/shard_map/all_gather | solution.py:24
  293.0 13.1 %fusion.466 = bf16[2,197,1024]{2,1,0:T(8,128)(2,1)} fusion(bf16[1,2048,1024]{2,1,0:T(8,128)(2,1)} %all-gather.37.cloned.1.call-done, f32[2,197,2048]{2,1,0:T(8,128)} %get-tuple-element.208, u8[197,2048]{1,0:T(8,128)(4,1)S(1)} %get-tuple-element.89, u8[197,2048]{1,0:T(8,128)(4,1)S(1)} %get-tuple-element.88), kind=kOutput, calls=%fused_computation.606 | convolution fusion | flops 1709443072 | bytes 9035776 | tf_op jit(solution)/shard_map/blf,fd->bld/dot_general | solution.py:156
  307.4 25.0 %all-gather.41.cloned.1.call-done = bf16[4,197,1024]{2,1,0:T(8,128)(2,1)} async-done(((bf16[2,197,1024]{2,1,0:T(8,128)(2,1)}), bf16[4,197,1024]{2,1,0:T(8,128)(2,1)}) %all-gather.41.cloned.1.call-update) | async-done | bytes 1613840 | tf_op jit(solution)/shard_map/all_gather | solution.py:65
  371.1 18.6 %all-gather.43.cloned.1.call-done = bf16[4,197,1024]{2,1,0:T(8,128)(2,1)} async-done(((bf16[2,197,1024]{2,1,0:T(8,128)(2,1)}), bf16[4,197,1024]{2,1,0:T(8,128)(2,1)}) %all-gather.43.cloned.1.call-update) | async-done | bytes 1613840 | tf_op jit(solution)/shard_map/all_gather | solution.py:65
  394.9 8.4 fusion.580
  403.3 4.4 convert_reduce_fusion.2
  413.5 12.8 %fusion.471 = bf16[2,197,1024]{2,1,0:T(8,128)(2,1)} fusion(bf16[1,2048,1024]{2,1,0:T(8,128)(2,1)} %all-gather.37.cloned.1.call-done, f32[2,197,2048]{2,1,0:T(8,128)} %get-tuple-element.211, u8[197,2048]{1,0:T(8,128)(4,1)} %get-tuple-element.160, u8[197,2048]{1,0:T(8,128)(4,1)} %get-tuple-element.161), kind=kOutput, calls=%fused_computation.607 | convolution fusion | flops 1709443072 | bytes 9035776 | tf_op jit(solution)/shard_map/blf,fd->bld/dot_general | solution.py:156
  426.8 12.9 %all-gather.51.cloned.1.call-done = bf16[4,197,1024]{2,1,0:T(8,128)(2,1)} async-done(((bf16[2,197,1024]{2,1,0:T(8,128)(2,1)}), bf16[4,197,1024]{2,1,0:T(8,128)(2,1)}) %all-gather.51.cloned.1.call-update) | async-done | bytes 1613840 | tf_op jit(solution)/shard_map/all_gather | solution.py:65
  453.4 4.4 convert_reduce_fusion.22
  457.8 3.7 multiply_reduce_fusion.2
  461.5 8.4 all-gather.45.cloned.1.call-done
  491.4 4.7 bitcast_convert_fusion.2
  527.1 27.1 %all-gather.47.cloned.1.call-done = bf16[4,197,1024]{2,1,0:T(8,128)(2,1)} async-done(((bf16[2,197,1024]{2,1,0:T(8,128)(2,1)}), bf16[4,197,1024]{2,1,0:T(8,128)(2,1)}) %all-gather.47.cloned.1.call-update) | async-done | bytes 1613840 | tf_op jit(solution)/shard_map/all_gather | solution.py:65
  558.8 5.4 fusion.844
  568.1 10.1 fusion.582
  579.3 5.2 convert_reduce_fusion.1
  589.0 3.7 fusion.621
  593.1 23.6 %all-gather.55.cloned.1.call-done = bf16[4,197,1024]{2,1,0:T(8,128)(2,1)} async-done(((bf16[2,197,1024]{2,1,0:T(8,128)(2,1)}), bf16[4,197,1024]{2,1,0:T(8,128)(2,1)}) %all-gather.55.cloned.1.call-update) | async-done | bytes 1613840 | tf_op jit(solution)/shard_map/all_gather | solution.py:65
  630.3 4.4 convert_reduce_fusion.20
  647.2 4.6 bitcast_convert_fusion.1
  652.8 27.2 %all-gather.57.cloned.1.call-done = bf16[4,197,1024]{2,1,0:T(8,128)(2,1)} async-done(((bf16[2,197,1024]{2,1,0:T(8,128)(2,1)}), bf16[4,197,1024]{2,1,0:T(8,128)(2,1)}) %all-gather.57.cloned.1.call-update) | async-done | bytes 1613840 | tf_op jit(solution)/shard_map/all_gather | solution.py:65
  703.1 12.9 %fusion.476 = bf16[2,197,1024]{2,1,0:T(8,128)(2,1)} fusion(bf16[1,2048,1024]{2,1,0:T(8,128)(2,1)} %all-gather.37.cloned.1.call-done, f32[2,197,2048]{2,1,0:T(8,128)} %get-tuple-element.216, u8[197,2048]{1,0:T(8,128)(4,1)} %get-tuple-element.158, u8[197,2048]{1,0:T(8,128)(4,1)} %get-tuple-element.159), kind=kOutput, calls=%fused_computation.608 | convolution fusion | flops 1709443072 | bytes 9035776 | tf_op jit(solution)/shard_map/blf,fd->bld/dot_general | solution.py:156
  716.4 15.5 %all-gather.59.cloned.1.call-done = bf16[4,197,1024]{2,1,0:T(8,128)(2,1)} async-done(((bf16[2,197,1024]{2,1,0:T(8,128)(2,1)}), bf16[4,197,1024]{2,1,0:T(8,128)(2,1)}) %all-gather.59.cloned.1.call-update) | async-done | bytes 1613840 | tf_op jit(solution)/shard_map/all_gather | solution.py:65
  745.7 4.9 multiply_reduce_fusion
  753.0 3.9 multiply_convert_fusion
  764.3 4.7 bitcast_convert_fusion
  781.0 3.9 copy.393
  794.0 4.1 fusion.101
  798.0 7.6 copy.391
  805.7 5.1 copy.404
  810.9 11.6 %fusion.169 = f32[2048,1024,1]{1,0,2:T(8,128)S(1)} fusion(f32[2,197,2048]{2,1,0:T(8,128)} %copy-done.163, u8[197,2048]{1,0:T(8,128)(4,1)S(1)} %copy-done.166, f32[2]{0:T(128)S(1)} %copy-done.147, bf16[1,2,197,1024]{3,1,2,0:T(2,128)(2,1)S(1)} %copy-done.72, pred[]{:T(512)S(6)} %eq.3), kind=kOutput, calls=%fused_computation.286 | convolution fusion | flops 1709039616 | bytes 12826633 | tf_op jit(solution)/shard_map/blf,bld->fd/dot_general | solution.py:186
  822.5 9.1 fusion.167
  831.6 10.6 fusion.100
  842.2 20.6 %copy.395 = bf16[1,2048,1024]{1,0,2:T(2,128)(2,1)} copy(bf16[1,2048,1024]{2,1,0:T(8,128)(2,1)} %fusion.100) | data formatting | bytes 8388608
  862.8 8.0 copy.517
  871.5 4.6 fusion.519
  876.2 5.9 fusion.520
  882.0 8.0 fusion.99
  900.9 3.8 fusion.526
  911.3 38.2 %all-reduce = f32[8,1152]{1,0:T(8,128)S(1)} all-reduce(f32[8,1152]{1,0:T(8,128)S(1)} %constant_dynamic-update-slice_fusion), channel_id=15, replica_groups=mesh['section'=2,'dp'=8,'mp'=2] {'dp'}, use_global_device_ids=true, to_apply=%region_84.85.clone | all-reduce | flops 9216 | bytes 73728
  957.9 75.2 %reduce-scatter.17.cloned.1.call-done = bf16[128,2048]{1,0:T(8,128)(2,1)} async-done(((bf16[1024,2048]{1,0:T(8,128)(2,1)}), bf16[128,2048]{1,0:T(8,128)(2,1)}) %reduce-scatter.17.cloned.1.call-update) | async-done | bytes 524304
  1036.7 87.9 %reduce-scatter.11.cloned.1.call-done = bf16[1,128,2048]{2,1,0:T(8,128)(2,1)} async-done(((bf16[1,1024,2048]{2,1,0:T(8,128)(2,1)}), bf16[1,128,2048]{2,1,0:T(8,128)(2,1)}) %reduce-scatter.11.cloned.1.call-update) | async-done | bytes 524304 | tf_op jit(solution)/shard_map/reduce_scatter | solution.py:58
  (619 shorter events, 292.5 us)
Async XLA Ops:
  7.2 65.9 %all-gather.31.cloned.1.call-start = ((), (), s32[]{:S(2)}) async-start(), calls=%async_computation.4 | async-start | bytes 3538944 | tf_op jit(solution)/shard_map/all_gather | solution.py:24
  7.9 105.3 %all-gather.33.cloned.1.call-start = ((), (), s32[]{:S(2)}) async-start(), calls=%async_computation.5 | async-start | bytes 1179648 | tf_op jit(solution)/shard_map/all_gather | solution.py:24
  8.7 134.5 %all-gather.39.cloned.1.call-start = ((), (), s32[]{:S(2)}) async-start(), calls=%async_computation.9 | async-start | bytes 2457600 | tf_op jit(solution)/shard_map/all_gather | solution.py:65
  49.0 27.7 %copy-start.136 = (f32[1024]{0:T(1024)}, f32[1024]{0:T(1024)S(1)}, u32[]{:S(2)}) copy-start(f32[1024]{0:T(1024)S(1)} %get-tuple-element.202) | copy-start | bytes 12292
  49.0 519.0 %copy-start.95 = (f32[1024]{0:T(1024)}, f32[1024]{0:T(1024)S(1)}, u32[]{:S(2)}) copy-start(f32[1024]{0:T(1024)S(1)} %get-tuple-element.200) | copy-start | bytes 12292
  51.5 290.1 %copy-start.64 = (bf16[1,2,197,1024]{3,1,2,0:T(2,128)(2,1)}, bf16[1,2,197,1024]{3,1,2,0:T(2,128)(2,1)S(1)}, u32[]{:S(2)}) copy-start(bf16[1,2,197,1024]{3,1,2,0:T(2,128)(2,1)S(1)} %get-tuple-element.181) | copy-start | bytes 2420740
  53.3 29.3 %copy-start.99 = (f32[8,64]{1,0:T(8,128)}, f32[8,64]{1,0:T(8,128)S(1)}, u32[]{:S(2)}) copy-start(f32[8,64]{1,0:T(8,128)S(1)} %add.590) | copy-start | bytes 6148
  86.5 29.5 %copy-start.50 = (bf16[2,197,8,64]{1,3,2,0:T(8,128)(2,1)}, bf16[2,197,8,64]{1,3,2,0:T(8,128)(2,1)S(1)}, u32[]{:S(2)}) copy-start(bf16[2,197,8,64]{1,3,2,0:T(8,128)(2,1)S(1)} %add_convert_fusion.13) | copy-start | bytes 1210372
  87.2 55.9 %copy-start.75 = (bf16[2,8,64,197]{3,2,1,0:T(8,128)(2,1)}, bf16[2,8,64,197]{3,2,1,0:T(8,128)(2,1)S(1)}, u32[]{:S(2)}) copy-start(bf16[2,8,64,197]{3,2,1,0:T(8,128)(2,1)S(1)} %fusion.490) | copy-start | bytes 1210372
  116.0 101.9 %all-gather.35.cloned.1.call-start = ((), (), s32[]{:S(2)}) async-start(), calls=%async_computation.6 | async-start | bytes 4718592 | tf_op jit(solution)/shard_map/all_gather | solution.py:24
  116.6 101.3 %copy-start.134 = (f32[1024]{0:T(1024)S(1)}, f32[1024]{0:T(1024)}, u32[]{:S(2)}) copy-start(f32[1024]{0:T(1024)} %get-tuple-element.198) | copy-start | bytes 12292
  116.6 176.4 %all-gather.37.cloned.1.call-start = ((), (), s32[]{:S(2)}) async-start(), calls=%async_computation.7 | async-start | bytes 4718592 | tf_op jit(solution)/shard_map/all_gather | solution.py:24
  117.2 215.2 %all-gather.41.cloned.1.call-start = ((), (), s32[]{:S(2)}) async-start(), calls=%async_computation.10 | async-start | bytes 2457600 | tf_op jit(solution)/shard_map/all_gather | solution.py:65
  293.0 13.2 %copy-start.145 = (s32[2,1]{0,1:T(1,128)S(1)}, s32[2,1]{0,1:T(1,128)}, u32[]{:S(2)}) copy-start(s32[2,1]{0,1:T(1,128)} %param.17) | copy-start | bytes 28
  306.1 29.2 %copy-start.101 = (f32[1024]{0:T(1024)S(1)}, f32[1024]{0:T(1024)}, u32[]{:S(2)}) copy-start(f32[1024]{0:T(1024)} %get-tuple-element.197) | copy-start | bytes 12292
  306.1 83.6 %all-gather.43.cloned.1.call-start = ((), (), s32[]{:S(2)}) async-start(), calls=%async_computation.11 | async-start | bytes 2457600 | tf_op jit(solution)/shard_map/all_gather | solution.py:65
  338.0 3.6 collective-permute-start
  355.9 11.6 %copy-start.19 = (bf16[1,2,197,512]{2,3,1,0:T(8,128)(2,1)}, bf16[1,2,197,512]{2,3,1,0:T(8,128)(2,1)S(1)}, u32[]{:S(2)}) copy-start(bf16[1,2,197,512]{2,3,1,0:T(8,128)(2,1)S(1)} %copy.319) | copy-start | bytes 1210372
  361.6 78.2 %all-gather.51.cloned.1.call-start = ((), (), s32[]{:S(2)}) async-start(), calls=%async_computation.15 | async-start | bytes 2457600 | tf_op jit(solution)/shard_map/all_gather | solution.py:65
  362.5 83.5 %copy-start.146 = (f32[2]{0:T(128)}, f32[2]{0:T(128)S(1)}, u32[]{:S(2)}) copy-start(f32[2]{0:T(128)S(1)} %broadcast_select_fusion.27) | copy-start | bytes 28
  391.8 81.0 %copy-start.17 = (bf16[2,197,1024]{2,1,0:T(8,128)(2,1)}, bf16[2,197,1024]{2,1,0:T(8,128)(2,1)S(1)}, u32[]{:S(2)}) copy-start(bf16[2,197,1024]{2,1,0:T(8,128)(2,1)S(1)} %reduce_sum.775) | copy-start | bytes 2420740
  411.7 58.2 %all-gather.45.cloned.1.call-start = ((), (), s32[]{:S(2)}) async-start(), calls=%async_computation.12 | async-start | bytes 2457600 | tf_op jit(solution)/shard_map/all_gather | solution.py:65
  411.8 34.2 %copy-start.103 = (f32[2,197]{1,0:T(2,128)}, f32[2,197]{1,0:T(2,128)S(1)}, u32[]{:S(2)}) copy-start(f32[2,197]{1,0:T(2,128)S(1)} %broadcast_multiply_fusion.17) | copy-start | bytes 4732
  413.5 32.4 %copy-start.107 = (f32[2,197]{1,0:T(2,128)}, f32[2,197]{1,0:T(2,128)S(1)}, u32[]{:S(2)}) copy-start(f32[2,197]{1,0:T(2,128)S(1)} %add_rsqrt_fusion.5) | copy-start | bytes 4732
  426.4 97.8 %all-gather.53.cloned.1.call-start = ((), (), s32[]{:S(2)}) async-start(), calls=%async_computation.16 | async-start | bytes 2457600 | tf_op jit(solution)/shard_map/all_gather | solution.py:65
  477.8 18.5 %collective-permute-start.1 = (bf16[2,197,1024]{2,0,1:T(2,128)(2,1)}, bf16[2,197,1024]{2,0,1:T(2,128)(2,1)}, u32[]{:S(2)}, u32[]{:S(2)}) collective-permute-start(bf16[2,197,1024]{2,0,1:T(2,128)(2,1)} %copy.322), channel_id=1, source_target_pairs={{0,16},{1,17},{2,18},{3,19},{4,20},{5,21},{6,22},{7,23},{8,24},{9,... | collective-permute-start | bytes 2420744 | tf_op jit(solution)/shard_map/ppermute | solution.py:71
  496.1 58.2 %all-gather.47.cloned.1.call-start = ((), (), s32[]{:S(2)}) async-start(), calls=%async_computation.13 | async-start | bytes 2457600 | tf_op jit(solution)/shard_map/all_gather | solution.py:65
  519.5 97.1 %all-gather.55.cloned.1.call-start = ((), (), s32[]{:S(2)}) async-start(), calls=%async_computation.17 | async-start | bytes 2457600 | tf_op jit(solution)/shard_map/all_gather | solution.py:65
  520.9 43.2 %copy-start.113 = (f32[2,197]{1,0:T(2,128)}, f32[2,197]{1,0:T(2,128)S(1)}, u32[]{:S(2)}) copy-start(f32[2,197]{1,0:T(2,128)S(1)} %add_rsqrt_fusion.4) | copy-start | bytes 4732
  565.4 12.8 %copy-start.60 = (bf16[2,197,1024]{2,1,0:T(8,128)(2,1)}, bf16[2,197,1024]{2,1,0:T(8,128)(2,1)S(1)}, u32[]{:S(2)}) copy-start(bf16[2,197,1024]{2,1,0:T(8,128)(2,1)S(1)} %get-tuple-element.187) | copy-start | bytes 2420740
  566.3 11.9 %copy-start.18 = (bf16[1,2,197,1024]{3,1,2,0:T(2,128)(2,1)S(1)}, bf16[1,2,197,1024]{3,1,2,0:T(2,128)(2,1)}, u32[]{:S(2)}) copy-start(bf16[1,2,197,1024]{3,1,2,0:T(2,128)(2,1)} %get-tuple-element.179) | copy-start | bytes 2420740
  566.3 13.0 %copy-start.149 = (bf16[1,2048,1024]{2,1,0:T(8,128)(2,1)S(1)}, bf16[1,2048,1024]{2,1,0:T(8,128)(2,1)}, u32[]{:S(2)}) copy-start(bf16[1,2048,1024]{2,1,0:T(8,128)(2,1)} %all-gather.37.cloned.1.call-done) | copy-start | bytes 12582916
  566.3 11.9 %collective-permute-start.2 = (bf16[2,197,1024]{2,0,1:T(2,128)(2,1)S(1)}, bf16[2,197,1024]{2,0,1:T(2,128)(2,1)S(1)}, u32[]{:S(2)}, u32[]{:S(2)}) collective-permute-start(bf16[2,197,1024]{2,0,1:T(2,128)(2,1)S(1)} %copy.337), channel_id=1, source_target_pairs={{16,0},{17,1},{18,2},{19,3},{20,4},{21,5},{22,6},{23,7},{24,8},{25... | collective-permute-start | bytes 2420744 | tf_op jit(solution)/shard_map/ppermute | solution.py:71
  588.6 91.4 %all-gather.57.cloned.1.call-start = ((), (), s32[]{:S(2)}) async-start(), calls=%async_computation.18 | async-start | bytes 2457600 | tf_op jit(solution)/shard_map/all_gather | solution.py:65
  592.8 30.0 %copy-start.105 = (f32[2,197]{1,0:T(2,128)}, f32[2,197]{1,0:T(2,128)S(1)}, u32[]{:S(2)}) copy-start(f32[2,197]{1,0:T(2,128)S(1)} %broadcast_multiply_fusion.11) | copy-start | bytes 4732
  593.1 32.7 %copy-start.109 = (f32[2,197]{1,0:T(2,128)}, f32[2,197]{1,0:T(2,128)S(1)}, u32[]{:S(2)}) copy-start(f32[2,197]{1,0:T(2,128)S(1)} %add_rsqrt_fusion.3) | copy-start | bytes 4732
  651.9 80.0 %all-gather.59.cloned.1.call-start = ((), (), s32[]{:S(2)}) async-start(), calls=%async_computation.19 | async-start | bytes 2457600 | tf_op jit(solution)/shard_map/all_gather | solution.py:65
  652.8 35.5 %copy-start.111 = (f32[2,197]{1,0:T(2,128)}, f32[2,197]{1,0:T(2,128)S(1)}, u32[]{:S(2)}) copy-start(f32[2,197]{1,0:T(2,128)S(1)} %add_rsqrt_fusion.2) | copy-start | bytes 4732
  689.2 4.2 collective-permute-start.3
  703.0 189.1 %all-gather.49.cloned.1.call-start = ((), (), s32[]{:S(2)}) async-start(), calls=%async_computation.14 | async-start | bytes 2457600 | tf_op jit(solution)/shard_map/all_gather | solution.py:65
  716.0 179.8 %all-gather.61.cloned.1.call-start = ((), (), s32[]{:S(2)}) async-start(), calls=%async_computation.20 | async-start | bytes 2457600 | tf_op jit(solution)/shard_map/all_gather | solution.py:65
  769.1 183.8 %reduce-scatter.15.cloned.1.call-start = ((), (), s32[]{:S(2)}) async-start(), calls=%async_computation.22 | async-start | bytes 1179648
  787.9 166.9 %reduce-scatter.13.cloned.1.call-start = ((), (), s32[]{:S(2)}) async-start(), calls=%async_computation.21 | async-start | bytes 3538944
  810.8 222.3 %reduce-scatter.17.cloned.1.call-start = ((), (), s32[]{:S(2)}) async-start(), calls=%async_computation.23 | async-start | bytes 4718592
  810.8 11.6 %copy-start.86 = (bf16[2,197,1024]{2,1,0:T(8,128)(2,1)S(1)}, bf16[2,197,1024]{2,1,0:T(8,128)(2,1)}, u32[]{:S(2)}) copy-start(bf16[2,197,1024]{2,1,0:T(8,128)(2,1)} %copy-done.85) | copy-start | bytes 2420740
  810.8 11.6 %copy-start.162 = (f32[2,197,2048]{2,1,0:T(8,128)S(1)}, f32[2,197,2048]{2,1,0:T(8,128)}, u32[]{:S(2)}) copy-start(f32[2,197,2048]{2,1,0:T(8,128)} %get-tuple-element.157) | copy-start | bytes 9682948
  810.9 11.6 %copy-start.165 = (u8[197,2048]{1,0:T(8,128)(4,1)S(1)}, u8[197,2048]{1,0:T(8,128)(4,1)}, u32[]{:S(2)}) copy-start(u8[197,2048]{1,0:T(8,128)(4,1)} %get-tuple-element.156) | copy-start | bytes 1210372
  870.9 253.7 %reduce-scatter.11.cloned.1.call-start = ((), (), s32[]{:S(2)}) async-start(), calls=%async_computation.8 | async-start | bytes 4718592 | tf_op jit(solution)/shard_map/reduce_scatter | solution.py:58
  (143 other events, 549.2 us)
Sparse Core Ops, SparseCore 0:
  10.2 62.8 all-gather.30
  75.1 38.1 all-gather.32
  116.1 26.9 all-gather.38
  145.1 72.7 all-gather.34
  219.8 73.1 all-gather.36
  306.3 26.1 all-gather.40
  361.7 27.9 all-gather.42
  411.8 27.9 all-gather.50
  441.9 27.9 all-gather.44
  496.2 27.9 all-gather.52
  526.3 27.9 all-gather.46
  588.7 27.9 all-gather.54
  652.0 27.9 all-gather.56
  703.1 28.7 all-gather.58
  733.3 27.9 all-gather.48
  769.2 27.8 all-gather.60
  800.9 64.0 reduce-scatter.14
  868.4 73.5 reduce-scatter.12
  945.6 87.4 reduce-scatter.16
  1036.6 87.9 reduce-scatter.10
